TPU v7x, 32 devices: a whole 2x2x4 slice. The times are simulated.
32 devices in a mesh: batch: 8 (over z, x), head: 4 (over y, core).
Axes of the slice: x: 2, y: 2, z: 4, core: 2. Of those that a mesh axis runs over, the one named last changes fastest.
Arguments:
- features: bfloat16 [1024, 24, 512], P(('batch', 'head')), may hold values from -6 to 6
- state_h: bfloat16 [1024, 1024], P(('batch', 'head')), may hold values from -0.8984375 to 0.8984375
- state_c: bfloat16 [1024, 1024], P(('batch', 'head')), may hold values from -4 to 4
- valid: int32 [1024], P(('batch', 'head')), may hold values 0 or 1
- ends: int32 [1024, 24], P(('batch', 'head')), may hold values 0 or 1
- policy: int32 [1024, 1], P(('batch', 'head')), may hold values from 0 to 31; in each aligned block of 32 rows (0 to 31, 32 to 63, ...) at most 2 rows name the same one
- actions: int32 [1024, 16], P(('batch', 'head')), may hold values from 0 to 17
- w_input: bfloat16 [512, 4, 1024], P('batch', None, 'head'), may hold values from -0.25 to 0.25
- w_recur: bfloat16 [1024, 4, 1024], P('batch', None, 'head'), may hold values from -0.1875 to 0.1875
- lstm_bias: float32 [4, 1024], replicated, may hold values from -3 to 5
- w_hidden: bfloat16 [32, 1024, 1024], P('head'), may hold values from -0.1875 to 0.1875
- w_value: bfloat16 [32, 512], P('head'), may hold values from -0.25 to 0.25
- w_advantage: bfloat16 [32, 512, 18], P('head'), may hold values from -0.25 to 0.25
Outputs:
- q_values: float32 [1024, 16, 18], P(('batch', 'head'))
- q_taken: float32 [1024, 16], P(('batch', 'head'))
Inputs may be any that keep to these rules, and one draw needn't show every extreme that they name: In the rows of one device no policy appears more than 2 times, and some policy appears exactly 2 times.
All inputs are finite; a program needn't handle non-finite values. No bound on the sum of `valid` or of `ends` on one device may be relied on, other than what follows from the above.
Results may differ from a plain program's by a relative error of at most 0.007.
Values may be sent and summed in bfloat16 or wider, within the bound.
No kernel may reach another device: no remote copies, remote signals or barrier semaphores. Data moves between devices by JAX's collectives and lax.ppermute only.
A program may use at most 128 MiB of HBM per device.

v0:
```python
import jax
import jax.numpy as jnp
from jax import lax
from jax.sharding import PartitionSpec as P

ACTIONS = 18
POLICIES = 32
CAPP = 2


def slot_table(owners, per_source, capacity, policies):
    count = owners.shape[0]
    sources = count // per_source
    place = jnp.arange(count, dtype=jnp.int32)
    anchor = place // per_source
    before = (
        (owners[:, None] == owners[None, :])
        & (anchor[:, None] == anchor[None, :])
        & (place[None, :] < place[:, None])
    )
    rank = jnp.sum(before.astype(jnp.int32), axis=1)
    target = owners * (sources * capacity) + anchor * capacity + rank
    total = policies * sources * capacity
    return (jnp.arange(total, dtype=jnp.int32)[:, None] == target[None, :]).astype(jnp.bfloat16)


def lstm_cell(pre_t, full_h, cell_state, keep_t, w_flat, bias, width):
    full_h = full_h * keep_t[:, None].astype(jnp.bfloat16)
    cell_state = cell_state * keep_t[:, None]
    gates = (
        pre_t
        + jnp.dot(full_h, w_flat, preferred_element_type=jnp.float32).reshape(-1, 4, width)
        + bias
    )
    cell_state = jax.nn.sigmoid(gates[:, 1]) * cell_state + jax.nn.sigmoid(gates[:, 0]) * jnp.tanh(
        gates[:, 2]
    )
    new_h = (jax.nn.sigmoid(gates[:, 3]) * jnp.tanh(cell_state)).astype(jnp.bfloat16)
    return (new_h, cell_state)


def shards(
    features,
    state_h,
    state_c,
    valid,
    ends,
    policy,
    actions,
    w_input,
    w_recur,
    lstm_bias,
    w_hidden,
    w_value,
    w_advantage,
):
    seq_dev, steps, width_e = features.shape
    width_h = state_h.shape[1]
    learn = actions.shape[1]
    burn = steps - learn
    heads_n = lax.axis_size("head")
    keep_start = valid.astype(jnp.bfloat16)[:, None]
    start_h = state_h * keep_start
    start_c = state_c * keep_start
    quarter = width_h // heads_n
    place = lax.axis_index("head")
    w_in_part, w_rec_part = (
        lax.all_gather(w_input, "batch", axis=0, tiled=True),
        lax.all_gather(w_recur, "batch", axis=0, tiled=True),
    )
    feats, ends_group, owners_group, group_h, group_c = (
        lax.all_gather(features, "head", axis=0, tiled=True),
        lax.all_gather(ends.astype(jnp.bfloat16), "head", axis=0, tiled=True),
        lax.all_gather(policy.astype(jnp.bfloat16), "head", axis=0, tiled=True),
        lax.all_gather(start_h, "head", axis=0, tiled=True),
        lax.all_gather(start_c, "head", axis=0, tiled=True),
    )
    group = feats.shape[0]
    pre = jnp.dot(
        feats.transpose(1, 0, 2).reshape(-1, width_e),
        w_in_part.reshape(width_e, 4 * quarter),
        preferred_element_type=jnp.float32,
    ).reshape(steps, group, 4, quarter)
    bias = lax.dynamic_slice_in_dim(lstm_bias, place * quarter, quarter, 1)
    part_h = lax.dynamic_slice_in_dim(group_h, place * quarter, quarter, 1)
    part_c = lax.dynamic_slice_in_dim(group_c, place * quarter, quarter, 1).astype(jnp.float32)
    w_flat = w_rec_part.reshape(width_h, 4 * quarter)
    keeps = 1.0 - ends_group.astype(jnp.float32).T

    def advance(carry, inputs):
        part_h, part_c = carry
        pre_t, keep_t = inputs
        full_h = lax.all_gather(part_h, "head", axis=1, tiled=True)
        new_h, part_c = lstm_cell(pre_t, full_h, part_c, keep_t, w_flat, bias, quarter)
        return ((new_h, part_c), new_h)

    _, outputs = lax.scan(advance, (part_h, part_c), (pre, keeps))
    learned = outputs[burn:]
    table = slot_table(owners_group[:, 0].astype(jnp.int32), seq_dev, CAPP, POLICIES)
    packed = jnp.einsum("ks,tsu->ktu", table, learned, preferred_element_type=jnp.float32).astype(
        jnp.bfloat16
    )
    packed = packed.reshape(POLICIES, heads_n * CAPP, learn, quarter)
    routed = lax.all_to_all(packed, "head", split_axis=0, concat_axis=3, tiled=True)
    local_heads, slots = (routed.shape[0], routed.shape[1])
    rows = routed.reshape(local_heads, slots * learn, width_h)
    mid = jnp.einsum("prh,phk->prk", rows, w_hidden, preferred_element_type=jnp.float32)
    mid = jnp.maximum(mid, 0.0).astype(jnp.bfloat16)
    branch = w_value.shape[1]
    value = jnp.einsum(
        "prk,pk->pr", mid[:, :, :branch], w_value, preferred_element_type=jnp.float32
    )
    advantage = jnp.einsum(
        "prk,pka->pra", mid[:, :, branch:], w_advantage, preferred_element_type=jnp.float32
    )
    q_local = value[:, :, None] + advantage - jnp.mean(advantage, axis=-1, keepdims=True)
    q_local = q_local.reshape(local_heads, slots, learn, ACTIONS)
    returned = lax.all_to_all(
        q_local.astype(jnp.bfloat16), "head", split_axis=1, concat_axis=0, tiled=True
    ).astype(q_local.dtype)
    own_table = slot_table(policy[:, 0], seq_dev, CAPP, POLICIES).astype(jnp.float32)
    q_values = jnp.dot(
        own_table.T,
        returned.reshape(POLICIES * CAPP, learn * ACTIONS),
        precision=lax.Precision.HIGHEST,
    ).reshape(seq_dev, learn, ACTIONS)
    chosen = actions[:, :, None] == jnp.arange(ACTIONS, dtype=jnp.int32)[None, None, :]
    q_taken = jnp.sum(jnp.where(chosen, q_values, 0.0), axis=-1)
    return (q_values, q_taken)


def solution(mesh):
    return jax.shard_map(
        shards,
        mesh=mesh,
        in_specs=(
            P(("batch", "head"), None, None),
            P(("batch", "head"), None),
            P(("batch", "head"), None),
            P(("batch", "head")),
            P(("batch", "head"), None),
            P(("batch", "head"), None),
            P(("batch", "head"), None),
            P("batch", None, "head"),
            P("batch", None, "head"),
            P(),
            P("head", None, None),
            P("head", None),
            P("head", None, None),
        ),
        out_specs=(P(("batch", "head"), None, None), P(("batch", "head"), None)),
        check_vma=False,
    )
```

profile of v0, /device:TPU:0, one launch (start us, length us, event | category | flops | bytes accessed | tf_op | source)
XLA Modules:
  0.0 445.9 jit_solution(649766315634340554)
XLA Ops:
  10.8 6.3 %all-gather = bf16[4,32,24]{1,2,0:T(8,128)(2,1)S(1)} all-gather(bf16[1,32,24]{1,2,0:T(8,128)(2,1)S(1)} %convert_bitcast_fusion.1), channel_id=1, replica_groups=mesh['batch'=8,'head'=4] {'head'}, dimensions={0}, use_global_device_ids=true | all-gather | bytes 7680 | tf_op jit(solution)/shard_map/all_gather | solution.py:73
  19.9 7.9 %all-reduce = bf16[128]{0:T(256)(128)(2,1)S(1)} all-reduce(bf16[128]{0:T(256)(128)(2,1)S(1)} %dynamic-update-slice), channel_id=1, replica_groups=mesh['batch'=8,'head'=4] {'head'}, use_global_device_ids=true, to_apply=%add | all-reduce | flops 128 | bytes 512
  28.8 5.8 %all_gather.26 = bf16[128,1024]{1,0:T(8,128)(2,1)S(1)} all-gather(bf16[32,1024]{1,0:T(8,128)(2,1)S(1)} %get-tuple-element.100), channel_id=1, replica_groups=mesh['batch'=8,'head'=4] {'head'}, dimensions={0}, use_global_device_ids=true | all-gather | bytes 327680 | tf_op jit(solution)/shard_map/all_gather | solution.py:76
  34.6 5.8 %all_gather.25 = bf16[128,1024]{1,0:T(8,128)(2,1)S(1)} all-gather(bf16[32,1024]{1,0:T(8,128)(2,1)S(1)} %get-tuple-element.101), channel_id=1, replica_groups=mesh['batch'=8,'head'=4] {'head'}, dimensions={0}, use_global_device_ids=true | all-gather | bytes 327680 | tf_op jit(solution)/shard_map/all_gather | solution.py:75
  41.3 11.8 %all-gather.7.cloned.1.call-done = bf16[512,4,256]{2,1,0:T(4,128)(2,1)} async-done(((bf16[64,4,256]{2,1,0:T(4,128)(2,1)}), bf16[512,4,256]{2,1,0:T(4,128)(2,1)}) %all-gather.7.cloned.1.call-update) | async-done | bytes 1048592 | tf_op jit(solution)/shard_map/all_gather | solution.py:68
  54.8 48.3 %all-gather.9.cloned.1.call-done = bf16[1024,4,256]{2,1,0:T(4,128)(2,1)} async-done(((bf16[128,4,256]{2,1,0:T(4,128)(2,1)}), bf16[1024,4,256]{2,1,0:T(4,128)(2,1)}) %all-gather.9.cloned.1.call-update) | async-done | bytes 2097168 | tf_op jit(solution)/shard_map/all_gather | solution.py:69
  105.2 26.6 %all-gather.5.cloned.1.call-done = bf16[128,24,512]{2,1,0:T(8,128)(2,1)} async-done(((bf16[32,24,512]{2,1,0:T(8,128)(2,1)}), bf16[128,24,512]{2,1,0:T(8,128)(2,1)}) %all-gather.5.cloned.1.call-update) | async-done | bytes 3145744 | tf_op jit(solution)/shard_map/all_gather | solution.py:72
  131.7 8.4 %fusion.22 = f32[24,128,4,256]{3,0,2,1:T(8,128)} fusion(bf16[128,24,512]{2,1,0:T(8,128)(2,1)} %all-gather.5.cloned.1.call-done, bf16[512,4,256]{0,2,1:T(8,128)(2,1)S(1)} %copy.72), kind=kOutput, calls=%fused_computation.32 | convolution fusion | flops 3221225472 | bytes 16777216 | tf_op jit(solution)/shard_map/dot_general | solution.py:79
  140.1 239.5 %while.14 = (s32[]{:T(128)}, bf16[128,256]{1,0:T(8,128)(2,1)S(1)}, f32[128,256]{1,0:T(8,128)S(1)}, bf16[24,128,256]{2,1,0:T(8,128)(2,1)}, f32[24,128,4,256]{3,0,...) while((s32[]{:T(128)}, bf16[128,256]{1,0:T(8,128)(2,1)S(1)}, ...), condition=%wide.region_3.4_spmd, body=%wide.region_2.3_spmd.sunk | while | flops 269320320 | bytes 6756965 | solution.py:97
  140.1 5.8 %all_gather.32 = bf16[128,1024]{1,0:T(8,128)(2,1)S(1)} all-gather(bf16[128,256]{1,0:T(8,128)(2,1)S(1)} %get-tuple-element.175), channel_id=1, replica_groups=mesh['batch'=8,'head'=4] {'head'}, dimensions={1}, use_global_device_ids=true | all-gather | bytes 327680 | tf_op jit(solution)/shard_map/while/body/eval_jaxpr/all_gather | solution.py:93
  146.4 2.7 constant_dynamic-slice_fusion.5
  150.0 5.8 %all_gather.32 = bf16[128,1024]{1,0:T(8,128)(2,1)S(1)} all-gather(bf16[128,256]{1,0:T(8,128)(2,1)S(1)} %get-tuple-element.175), channel_id=1, replica_groups=mesh['batch'=8,'head'=4] {'head'}, dimensions={1}, use_global_device_ids=true | all-gather | bytes 327680 | tf_op jit(solution)/shard_map/while/body/eval_jaxpr/all_gather | solution.py:93
  156.4 2.7 constant_dynamic-slice_fusion.5
  160.0 5.8 %all_gather.32 = bf16[128,1024]{1,0:T(8,128)(2,1)S(1)} all-gather(bf16[128,256]{1,0:T(8,128)(2,1)S(1)} %get-tuple-element.175), channel_id=1, replica_groups=mesh['batch'=8,'head'=4] {'head'}, dimensions={1}, use_global_device_ids=true | all-gather | bytes 327680 | tf_op jit(solution)/shard_map/while/body/eval_jaxpr/all_gather | solution.py:93
  166.3 2.7 constant_dynamic-slice_fusion.5
  170.0 5.8 %all_gather.32 = bf16[128,1024]{1,0:T(8,128)(2,1)S(1)} all-gather(bf16[128,256]{1,0:T(8,128)(2,1)S(1)} %get-tuple-element.175), channel_id=1, replica_groups=mesh['batch'=8,'head'=4] {'head'}, dimensions={1}, use_global_device_ids=true | all-gather | bytes 327680 | tf_op jit(solution)/shard_map/while/body/eval_jaxpr/all_gather | solution.py:93
  176.3 2.7 constant_dynamic-slice_fusion.5
  180.0 5.8 %all_gather.32 = bf16[128,1024]{1,0:T(8,128)(2,1)S(1)} all-gather(bf16[128,256]{1,0:T(8,128)(2,1)S(1)} %get-tuple-element.175), channel_id=1, replica_groups=mesh['batch'=8,'head'=4] {'head'}, dimensions={1}, use_global_device_ids=true | all-gather | bytes 327680 | tf_op jit(solution)/shard_map/while/body/eval_jaxpr/all_gather | solution.py:93
  186.3 2.7 constant_dynamic-slice_fusion.5
  190.0 5.8 %all_gather.32 = bf16[128,1024]{1,0:T(8,128)(2,1)S(1)} all-gather(bf16[128,256]{1,0:T(8,128)(2,1)S(1)} %get-tuple-element.175), channel_id=1, replica_groups=mesh['batch'=8,'head'=4] {'head'}, dimensions={1}, use_global_device_ids=true | all-gather | bytes 327680 | tf_op jit(solution)/shard_map/while/body/eval_jaxpr/all_gather | solution.py:93
  196.3 2.7 constant_dynamic-slice_fusion.5
  199.9 5.8 %all_gather.32 = bf16[128,1024]{1,0:T(8,128)(2,1)S(1)} all-gather(bf16[128,256]{1,0:T(8,128)(2,1)S(1)} %get-tuple-element.175), channel_id=1, replica_groups=mesh['batch'=8,'head'=4] {'head'}, dimensions={1}, use_global_device_ids=true | all-gather | bytes 327680 | tf_op jit(solution)/shard_map/while/body/eval_jaxpr/all_gather | solution.py:93
  206.3 2.7 constant_dynamic-slice_fusion.5
  209.9 5.8 %all_gather.32 = bf16[128,1024]{1,0:T(8,128)(2,1)S(1)} all-gather(bf16[128,256]{1,0:T(8,128)(2,1)S(1)} %get-tuple-element.175), channel_id=1, replica_groups=mesh['batch'=8,'head'=4] {'head'}, dimensions={1}, use_global_device_ids=true | all-gather | bytes 327680 | tf_op jit(solution)/shard_map/while/body/eval_jaxpr/all_gather | solution.py:93
  216.3 2.7 constant_dynamic-slice_fusion.5
  219.9 5.8 %all_gather.32 = bf16[128,1024]{1,0:T(8,128)(2,1)S(1)} all-gather(bf16[128,256]{1,0:T(8,128)(2,1)S(1)} %get-tuple-element.175), channel_id=1, replica_groups=mesh['batch'=8,'head'=4] {'head'}, dimensions={1}, use_global_device_ids=true | all-gather | bytes 327680 | tf_op jit(solution)/shard_map/while/body/eval_jaxpr/all_gather | solution.py:93
  226.2 2.7 constant_dynamic-slice_fusion.5
  229.9 5.8 %all_gather.32 = bf16[128,1024]{1,0:T(8,128)(2,1)S(1)} all-gather(bf16[128,256]{1,0:T(8,128)(2,1)S(1)} %get-tuple-element.175), channel_id=1, replica_groups=mesh['batch'=8,'head'=4] {'head'}, dimensions={1}, use_global_device_ids=true | all-gather | bytes 327680 | tf_op jit(solution)/shard_map/while/body/eval_jaxpr/all_gather | solution.py:93
  236.2 2.7 constant_dynamic-slice_fusion.5
  239.9 5.8 %all_gather.32 = bf16[128,1024]{1,0:T(8,128)(2,1)S(1)} all-gather(bf16[128,256]{1,0:T(8,128)(2,1)S(1)} %get-tuple-element.175), channel_id=1, replica_groups=mesh['batch'=8,'head'=4] {'head'}, dimensions={1}, use_global_device_ids=true | all-gather | bytes 327680 | tf_op jit(solution)/shard_map/while/body/eval_jaxpr/all_gather | solution.py:93
  246.2 2.7 constant_dynamic-slice_fusion.5
  249.9 5.8 %all_gather.32 = bf16[128,1024]{1,0:T(8,128)(2,1)S(1)} all-gather(bf16[128,256]{1,0:T(8,128)(2,1)S(1)} %get-tuple-element.175), channel_id=1, replica_groups=mesh['batch'=8,'head'=4] {'head'}, dimensions={1}, use_global_device_ids=true | all-gather | bytes 327680 | tf_op jit(solution)/shard_map/while/body/eval_jaxpr/all_gather | solution.py:93
  256.2 2.7 constant_dynamic-slice_fusion.5
  259.9 5.8 %all_gather.32 = bf16[128,1024]{1,0:T(8,128)(2,1)S(1)} all-gather(bf16[128,256]{1,0:T(8,128)(2,1)S(1)} %get-tuple-element.175), channel_id=1, replica_groups=mesh['batch'=8,'head'=4] {'head'}, dimensions={1}, use_global_device_ids=true | all-gather | bytes 327680 | tf_op jit(solution)/shard_map/while/body/eval_jaxpr/all_gather | solution.py:93
  266.2 2.7 constant_dynamic-slice_fusion.5
  269.9 5.8 %all_gather.32 = bf16[128,1024]{1,0:T(8,128)(2,1)S(1)} all-gather(bf16[128,256]{1,0:T(8,128)(2,1)S(1)} %get-tuple-element.175), channel_id=1, replica_groups=mesh['batch'=8,'head'=4] {'head'}, dimensions={1}, use_global_device_ids=true | all-gather | bytes 327680 | tf_op jit(solution)/shard_map/while/body/eval_jaxpr/all_gather | solution.py:93
  276.2 2.7 constant_dynamic-slice_fusion.5
  279.8 5.8 %all_gather.32 = bf16[128,1024]{1,0:T(8,128)(2,1)S(1)} all-gather(bf16[128,256]{1,0:T(8,128)(2,1)S(1)} %get-tuple-element.175), channel_id=1, replica_groups=mesh['batch'=8,'head'=4] {'head'}, dimensions={1}, use_global_device_ids=true | all-gather | bytes 327680 | tf_op jit(solution)/shard_map/while/body/eval_jaxpr/all_gather | solution.py:93
  286.2 2.7 constant_dynamic-slice_fusion.5
  289.8 5.8 %all_gather.32 = bf16[128,1024]{1,0:T(8,128)(2,1)S(1)} all-gather(bf16[128,256]{1,0:T(8,128)(2,1)S(1)} %get-tuple-element.175), channel_id=1, replica_groups=mesh['batch'=8,'head'=4] {'head'}, dimensions={1}, use_global_device_ids=true | all-gather | bytes 327680 | tf_op jit(solution)/shard_map/while/body/eval_jaxpr/all_gather | solution.py:93
  296.1 2.7 constant_dynamic-slice_fusion.5
  299.8 5.8 %all_gather.32 = bf16[128,1024]{1,0:T(8,128)(2,1)S(1)} all-gather(bf16[128,256]{1,0:T(8,128)(2,1)S(1)} %get-tuple-element.175), channel_id=1, replica_groups=mesh['batch'=8,'head'=4] {'head'}, dimensions={1}, use_global_device_ids=true | all-gather | bytes 327680 | tf_op jit(solution)/shard_map/while/body/eval_jaxpr/all_gather | solution.py:93
  306.1 2.7 constant_dynamic-slice_fusion.5
  309.8 5.8 %all_gather.32 = bf16[128,1024]{1,0:T(8,128)(2,1)S(1)} all-gather(bf16[128,256]{1,0:T(8,128)(2,1)S(1)} %get-tuple-element.175), channel_id=1, replica_groups=mesh['batch'=8,'head'=4] {'head'}, dimensions={1}, use_global_device_ids=true | all-gather | bytes 327680 | tf_op jit(solution)/shard_map/while/body/eval_jaxpr/all_gather | solution.py:93
  316.1 2.7 constant_dynamic-slice_fusion.5
  319.8 5.8 %all_gather.32 = bf16[128,1024]{1,0:T(8,128)(2,1)S(1)} all-gather(bf16[128,256]{1,0:T(8,128)(2,1)S(1)} %get-tuple-element.175), channel_id=1, replica_groups=mesh['batch'=8,'head'=4] {'head'}, dimensions={1}, use_global_device_ids=true | all-gather | bytes 327680 | tf_op jit(solution)/shard_map/while/body/eval_jaxpr/all_gather | solution.py:93
  326.1 2.7 constant_dynamic-slice_fusion.5
  329.8 5.8 %all_gather.32 = bf16[128,1024]{1,0:T(8,128)(2,1)S(1)} all-gather(bf16[128,256]{1,0:T(8,128)(2,1)S(1)} %get-tuple-element.175), channel_id=1, replica_groups=mesh['batch'=8,'head'=4] {'head'}, dimensions={1}, use_global_device_ids=true | all-gather | bytes 327680 | tf_op jit(solution)/shard_map/while/body/eval_jaxpr/all_gather | solution.py:93
  336.1 2.7 constant_dynamic-slice_fusion.5
  339.7 5.8 %all_gather.32 = bf16[128,1024]{1,0:T(8,128)(2,1)S(1)} all-gather(bf16[128,256]{1,0:T(8,128)(2,1)S(1)} %get-tuple-element.175), channel_id=1, replica_groups=mesh['batch'=8,'head'=4] {'head'}, dimensions={1}, use_global_device_ids=true | all-gather | bytes 327680 | tf_op jit(solution)/shard_map/while/body/eval_jaxpr/all_gather | solution.py:93
  346.1 2.7 constant_dynamic-slice_fusion.5
  349.7 5.8 %all_gather.32 = bf16[128,1024]{1,0:T(8,128)(2,1)S(1)} all-gather(bf16[128,256]{1,0:T(8,128)(2,1)S(1)} %get-tuple-element.175), channel_id=1, replica_groups=mesh['batch'=8,'head'=4] {'head'}, dimensions={1}, use_global_device_ids=true | all-gather | bytes 327680 | tf_op jit(solution)/shard_map/while/body/eval_jaxpr/all_gather | solution.py:93
  356.1 2.7 constant_dynamic-slice_fusion.5
  359.7 5.8 %all_gather.32 = bf16[128,1024]{1,0:T(8,128)(2,1)S(1)} all-gather(bf16[128,256]{1,0:T(8,128)(2,1)S(1)} %get-tuple-element.175), channel_id=1, replica_groups=mesh['batch'=8,'head'=4] {'head'}, dimensions={1}, use_global_device_ids=true | all-gather | bytes 327680 | tf_op jit(solution)/shard_map/while/body/eval_jaxpr/all_gather | solution.py:93
  366.0 2.7 constant_dynamic-slice_fusion.5
  369.7 5.8 %all_gather.32 = bf16[128,1024]{1,0:T(8,128)(2,1)S(1)} all-gather(bf16[128,256]{1,0:T(8,128)(2,1)S(1)} %get-tuple-element.175), channel_id=1, replica_groups=mesh['batch'=8,'head'=4] {'head'}, dimensions={1}, use_global_device_ids=true | all-gather | bytes 327680 | tf_op jit(solution)/shard_map/while/body/eval_jaxpr/all_gather | solution.py:93
  376.0 2.7 constant_dynamic-slice_fusion.5
  383.2 3.9 all-to-all-start
  387.3 25.3 %all-to-all-done = bf16[32,8,16,256]{3,1,2,0:T(8,128)(2,1)S(1)} async-done(((bf16[32,8,16,256]{3,1,2,0:T(8,128)(2,1)}), bf16[32,8,16,256]{3,1,2,0:T(8,128)(2,1)S(1)}, u32[]{:S(2)}, u32[]{:S(2)}) %all-to-all-start) | async-done | bytes 2097184 | tf_op jit(solution)/shard_map/all_to_all | solution.py:104
  412.6 3.0 copy.91
  415.5 3.2 reshape.154
  418.8 8.2 %maximum_convert_fusion = bf16[8,128,1024]{2,1,0:T(8,128)(2,1)S(1)} fusion(bf16[8,128,1024]{2,1,0:T(8,128)(2,1)S(1)} %reshape.154, bf16[8,1024,1024]{2,1,0:T(8,128)(2,1)} %param.25), kind=kOutput, calls=%fused_computation.31 | convolution fusion | flops 2149580800 | bytes 20971520 | tf_op jit(solution)/shard_map/prh,phk->prk/dot_general | solution.py:107
  429.6 3.3 all-to-all-start.1
  432.9 3.9 all-to-all-done.1
  (149 shorter events, 53.9 us)
Async XLA Ops:
  7.2 419.8 %copy-start = (bf16[8,512,18]{1,0,2:T(8,128)(2,1)S(1)}, bf16[8,512,18]{1,0,2:T(8,128)(2,1)}, u32[]{:S(2)}) copy-start(bf16[8,512,18]{1,0,2:T(8,128)(2,1)} %param.27) | copy-start | bytes 442372
  7.2 46.0 %all-gather.7.cloned.1.call-start = ((), (), s32[]{:S(2)}) async-start(), calls=%async_computation.3 | async-start | bytes 1179648 | tf_op jit(solution)/shard_map/all_gather | solution.py:68
  7.9 95.2 %all-gather.9.cloned.1.call-start = ((), (), s32[]{:S(2)}) async-start(), calls=%async_computation.4 | async-start | bytes 2359296 | tf_op jit(solution)/shard_map/all_gather | solution.py:69
  8.7 123.1 %all-gather.5.cloned.1.call-start = ((), (), s32[]{:S(2)}) async-start(), calls=%async_computation.2 | async-start | bytes 3932160 | tf_op jit(solution)/shard_map/all_gather | solution.py:72
  383.2 3.9 copy-start.2
  383.2 29.4 %all-to-all-start = ((bf16[32,8,16,256]{3,1,2,0:T(8,128)(2,1)}), bf16[32,8,16,256]{3,1,2,0:T(8,128)(2,1)S(1)}, u32[]{:S(2)}, u32[]{:S(2)}) async-start(bf16[32,8,16,256]{3,1,2,0:T(8,128)(2,1)} %copy.61), calls=%async_computation | async-start | bytes 4194304 | tf_op jit(solution)/shard_map/all_to_all | solution.py:104
  418.8 8.6 %copy-start.3 = (bf16[8,512]{1,0:T(8,128)(2,1)S(1)}, bf16[8,512]{1,0:T(8,128)(2,1)}, u32[]{:S(2)}) copy-start(bf16[8,512]{1,0:T(8,128)(2,1)} %param.26) | copy-start | bytes 24580
  427.4 10.4 %copy-start.1 = (s32[32,16]{0,1:T(8,128)S(1)}, s32[32,16]{0,1:T(8,128)}, u32[]{:S(2)}) copy-start(s32[32,16]{0,1:T(8,128)} %param.21) | copy-start | bytes 6148
  429.6 7.2 %all-to-all-start.1 = ((bf16[4,2,2304]{2,1,0:T(2,128)(2,1)}), bf16[4,2,2304]{2,1,0:T(2,128)(2,1)S(1)}, u32[]{:S(2)}, u32[]{:S(2)}) async-start(bf16[4,2,2304]{2,1,0:T(2,128)(2,1)} %reshape.177), calls=%async_computation.1 | async-start | bytes 73728 | tf_op jit(solution)/shard_map/all_to_all | solution.py:118
Sparse Core Ops, SparseCore 0:
  10.1 42.9 all-gather.6
  55.3 47.7 all-gather.8
  104.7 27.0 all-gather.4
where the time goes:
time: 448 us; the launch traced here: 446 us
  blocking collectives  166 us (37%)
  waiting for transfers between devices  118 us (26%)
  local copies, waits for them, and re-layouts  82.5 us (18%)
  matrix products  31.8 us (7%)
  other arithmetic  25.4 us (6%)
  between operations  14.6 us (3%)
  starting transfers between devices  7.3 us (2%)
    all_gather x24, blocking collectives, advance(): full_h = lax.all_gather(part_h, 'head', axis=1, tiled=True)  140 us
    dynamic_slice x24, local copies, waits for them, and re-layouts, shards(): _, outputs = lax.scan(advance, (part_h, part_c), (pre, keeps))  65.2 us
    all_gather x1, waiting for transfers between devices, shards(): lax.all_gather(w_recur, 'batch', axis=0, tiled=True)  48.3 us
    all_gather x1, waiting for transfers between devices, shards(): lax.all_gather(features, 'head', axis=0, tiled=True)  26.6 us
    all_to_all x1, waiting for transfers between devices, shards(): lax.all_to_all(packed, 'head', split_axis=0, concat_axis=3, tiled=True)  25.3 us
    dynamic_update_slice x24, other arithmetic, shards(): _, outputs = lax.scan(advance, (part_h, part_c), (pre, keeps))  19.1 us
    all_gather x1, waiting for transfers between devices, shards(): lax.all_gather(w_input, 'batch', axis=0, tiled=True)  11.8 us
    dot_general x24, matrix products, lstm_cell(): jnp.dot(full_h, w_flat, preferred_element_type=jnp.float32)  11.7 us
  transfers between devices with their start and end apart: 5, of which 5 were waited for; matrix products, arithmetic and copies ran while one was open for 2% of the time, Pallas kernels for 0%

commit v1 on v0

--- a/solution.py
+++ b/solution.py
@@ -90,7 +90,8 @@
     def advance(carry, inputs):
         part_h, part_c = carry
         pre_t, keep_t = inputs
-        full_h = lax.all_gather(part_h, "head", axis=1, tiled=True)
+        parts = lax.all_gather(part_h, "head", axis=0, tiled=False)
+        full_h = jnp.concatenate(parts, axis=1)
         new_h, part_c = lstm_cell(pre_t, full_h, part_c, keep_t, w_flat, bias, quarter)
         return ((new_h, part_c), new_h)
 

time: 448 us -> 425 us (0.949)
  local copies, waits for them, and re-layouts: 82.5 us -> 27.2 us
  matrix products: 31.8 us -> 65.5 us
    dynamic_slice x24 -> x0, local copies, waits for them, and re-layouts: 65.2 us -> none  [shards(): _, outputs = lax.scan(advance, (part_h, part_c), (pre, keeps))]
    dot_general x24, matrix products: 11.7 us -> 45.1 us  [lstm_cell(): jnp.dot(full_h, w_flat, preferred_element_type=jnp.float32)]
    mul x0 -> x48, local copies, waits for them, and re-layouts: none -> 9.06 us  [lstm_cell(): full_h = full_h * keep_t[:, None].astype(jnp.bfloat16)]
where the time goes in v1:
time: 425 us; the launch traced here: 423 us
  blocking collectives  166 us (39%)
  waiting for transfers between devices  117 us (28%)
  matrix products  65.5 us (15%)
  local copies, waits for them, and re-layouts  27.2 us (6%)
  other arithmetic  24.8 us (6%)
  between operations  14.6 us (3%)
  starting transfers between devices  7.3 us (2%)
    all_gather x24, blocking collectives, advance(): parts = lax.all_gather(part_h, 'head', axis=0, tiled=False)  140 us
    all_gather x1, waiting for transfers between devices, shards(): lax.all_gather(w_recur, 'batch', axis=0, tiled=True)  48.3 us
    dot_general x24, matrix products, lstm_cell(): jnp.dot(full_h, w_flat, preferred_element_type=jnp.float32)  45.1 us
    all_gather x1, waiting for transfers between devices, shards(): lax.all_gather(features, 'head', axis=0, tiled=True)  25.7 us
    all_to_all x1, waiting for transfers between devices, shards(): lax.all_to_all(packed, 'head', split_axis=0, concat_axis=3, tiled=True)  25.3 us
    dynamic_update_slice x24, other arithmetic, shards(): _, outputs = lax.scan(advance, (part_h, part_c), (pre, keeps))  19.2 us
    all_gather x1, waiting for transfers between devices, shards(): lax.all_gather(w_input, 'batch', axis=0, tiled=True)  11.8 us
    mul x48, local copies, waits for them, and re-layouts, lstm_cell(): full_h = full_h * keep_t[:, None].astype(jnp.bfloat16)  9.06 us
  transfers between devices with their start and end apart: 5, of which 5 were waited for; matrix products, arithmetic and copies ran while one was open for 2% of the time, Pallas kernels for 0%

profile of v1, /device:TPU:0, one launch (start us, length us, event | category | flops | bytes accessed | tf_op | source)
XLA Modules:
  0.0 422.9 jit_solution(15213633172910885321)
XLA Ops:
  10.8 6.3 %all-gather.1 = bf16[4,32,24]{1,2,0:T(8,128)(2,1)S(1)} all-gather(bf16[1,32,24]{1,2,0:T(8,128)(2,1)S(1)} %convert_bitcast_fusion.1), channel_id=1, replica_groups=mesh['batch'=8,'head'=4] {'head'}, dimensions={0}, use_global_device_ids=true | all-gather | bytes 7680 | tf_op jit(solution)/shard_map/all_gather | solution.py:73
  19.9 7.9 %all-reduce = bf16[128]{0:T(256)(128)(2,1)S(1)} all-reduce(bf16[128]{0:T(256)(128)(2,1)S(1)} %dynamic-update-slice), channel_id=1, replica_groups=mesh['batch'=8,'head'=4] {'head'}, use_global_device_ids=true, to_apply=%add | all-reduce | flops 128 | bytes 512
  28.8 5.8 %all_gather.29 = bf16[128,1024]{1,0:T(8,128)(2,1)S(1)} all-gather(bf16[32,1024]{1,0:T(8,128)(2,1)S(1)} %get-tuple-element.100), channel_id=1, replica_groups=mesh['batch'=8,'head'=4] {'head'}, dimensions={0}, use_global_device_ids=true | all-gather | bytes 327680 | tf_op jit(solution)/shard_map/all_gather | solution.py:76
  34.6 5.8 %all_gather.28 = bf16[128,1024]{1,0:T(8,128)(2,1)S(1)} all-gather(bf16[32,1024]{1,0:T(8,128)(2,1)S(1)} %get-tuple-element.101), channel_id=1, replica_groups=mesh['batch'=8,'head'=4] {'head'}, dimensions={0}, use_global_device_ids=true | all-gather | bytes 327680 | tf_op jit(solution)/shard_map/all_gather | solution.py:75
  41.3 11.8 %all-gather.10.cloned.1.call-done = bf16[512,4,256]{2,1,0:T(4,128)(2,1)} async-done(((bf16[64,4,256]{2,1,0:T(4,128)(2,1)}), bf16[512,4,256]{2,1,0:T(4,128)(2,1)}) %all-gather.10.cloned.1.call-update) | async-done | bytes 1048592 | tf_op jit(solution)/shard_map/all_gather | solution.py:68
  54.8 48.3 %all-gather.12.cloned.1.call-done = bf16[1024,4,256]{2,1,0:T(4,128)(2,1)} async-done(((bf16[128,4,256]{2,1,0:T(4,128)(2,1)}), bf16[1024,4,256]{2,1,0:T(4,128)(2,1)}) %all-gather.12.cloned.1.call-update) | async-done | bytes 2097168 | tf_op jit(solution)/shard_map/all_gather | solution.py:69
  103.1 3.0 copy.73
  106.1 25.7 %all-gather.8.cloned.1.call-done = bf16[128,24,512]{2,1,0:T(8,128)(2,1)} async-done(((bf16[32,24,512]{2,1,0:T(8,128)(2,1)}), bf16[128,24,512]{2,1,0:T(8,128)(2,1)}) %all-gather.8.cloned.1.call-update) | async-done | bytes 3145744 | tf_op jit(solution)/shard_map/all_gather | solution.py:72
  131.7 8.7 %fusion.19 = f32[24,128,4,256]{3,1,2,0:T(8,128)} fusion(bf16[128,24,512]{2,1,0:T(8,128)(2,1)} %all-gather.8.cloned.1.call-done, bf16[512,4,256]{0,2,1:T(8,128)(2,1)S(1)} %copy.72), kind=kOutput, calls=%fused_computation.28 | convolution fusion | flops 3221225472 | bytes 16777216 | tf_op jit(solution)/shard_map/dot_general | solution.py:79
  140.5 216.2 %while.14 = (s32[]{:T(128)}, bf16[128,256]{1,0:T(8,128)(2,1)S(1)}, f32[128,256]{1,0:T(8,128)S(1)}, bf16[24,128,256]{2,1,0:T(8,128)(2,1)}, f32[24,128,4,256]{3,1,...) while((s32[]{:T(128)}, bf16[128,256]{1,0:T(8,128)(2,1)S(1)}, ...), condition=%wide.region_3.4_spmd, body=%wide.region_2.3_spmd.sunk | while | flops 269320320 | bytes 6232677 | solution.py:98
  140.5 5.8 %all-gather.3 = bf16[512,256]{1,0:T(8,128)(2,1)S(1)} all-gather(bf16[128,256]{1,0:T(8,128)(2,1)S(1)} %get-tuple-element.175), channel_id=2, replica_groups=mesh['batch'=8,'head'=4] {'head'}, dimensions={0}, use_global_device_ids=true | all-gather | bytes 327680 | tf_op jit(solution)/shard_map/while/body/eval_jaxpr/all_gather | solution.py:93
  146.7 1.9 fusion.56
  149.4 5.8 %all-gather.3 = bf16[512,256]{1,0:T(8,128)(2,1)S(1)} all-gather(bf16[128,256]{1,0:T(8,128)(2,1)S(1)} %get-tuple-element.175), channel_id=2, replica_groups=mesh['batch'=8,'head'=4] {'head'}, dimensions={0}, use_global_device_ids=true | all-gather | bytes 327680 | tf_op jit(solution)/shard_map/while/body/eval_jaxpr/all_gather | solution.py:93
  155.7 1.9 fusion.56
  158.4 5.8 %all-gather.3 = bf16[512,256]{1,0:T(8,128)(2,1)S(1)} all-gather(bf16[128,256]{1,0:T(8,128)(2,1)S(1)} %get-tuple-element.175), channel_id=2, replica_groups=mesh['batch'=8,'head'=4] {'head'}, dimensions={0}, use_global_device_ids=true | all-gather | bytes 327680 | tf_op jit(solution)/shard_map/while/body/eval_jaxpr/all_gather | solution.py:93
  164.7 1.9 fusion.56
  167.4 5.8 %all-gather.3 = bf16[512,256]{1,0:T(8,128)(2,1)S(1)} all-gather(bf16[128,256]{1,0:T(8,128)(2,1)S(1)} %get-tuple-element.175), channel_id=2, replica_groups=mesh['batch'=8,'head'=4] {'head'}, dimensions={0}, use_global_device_ids=true | all-gather | bytes 327680 | tf_op jit(solution)/shard_map/while/body/eval_jaxpr/all_gather | solution.py:93
  173.7 1.9 fusion.56
  176.4 5.8 %all-gather.3 = bf16[512,256]{1,0:T(8,128)(2,1)S(1)} all-gather(bf16[128,256]{1,0:T(8,128)(2,1)S(1)} %get-tuple-element.175), channel_id=2, replica_groups=mesh['batch'=8,'head'=4] {'head'}, dimensions={0}, use_global_device_ids=true | all-gather | bytes 327680 | tf_op jit(solution)/shard_map/while/body/eval_jaxpr/all_gather | solution.py:93
  182.8 1.9 fusion.56
  185.4 5.8 %all-gather.3 = bf16[512,256]{1,0:T(8,128)(2,1)S(1)} all-gather(bf16[128,256]{1,0:T(8,128)(2,1)S(1)} %get-tuple-element.175), channel_id=2, replica_groups=mesh['batch'=8,'head'=4] {'head'}, dimensions={0}, use_global_device_ids=true | all-gather | bytes 327680 | tf_op jit(solution)/shard_map/while/body/eval_jaxpr/all_gather | solution.py:93
  191.8 1.9 fusion.56
  194.4 5.8 %all-gather.3 = bf16[512,256]{1,0:T(8,128)(2,1)S(1)} all-gather(bf16[128,256]{1,0:T(8,128)(2,1)S(1)} %get-tuple-element.175), channel_id=2, replica_groups=mesh['batch'=8,'head'=4] {'head'}, dimensions={0}, use_global_device_ids=true | all-gather | bytes 327680 | tf_op jit(solution)/shard_map/while/body/eval_jaxpr/all_gather | solution.py:93
  200.8 1.9 fusion.56
  203.4 5.8 %all-gather.3 = bf16[512,256]{1,0:T(8,128)(2,1)S(1)} all-gather(bf16[128,256]{1,0:T(8,128)(2,1)S(1)} %get-tuple-element.175), channel_id=2, replica_groups=mesh['batch'=8,'head'=4] {'head'}, dimensions={0}, use_global_device_ids=true | all-gather | bytes 327680 | tf_op jit(solution)/shard_map/while/body/eval_jaxpr/all_gather | solution.py:93
  209.8 1.9 fusion.56
  212.4 5.8 %all-gather.3 = bf16[512,256]{1,0:T(8,128)(2,1)S(1)} all-gather(bf16[128,256]{1,0:T(8,128)(2,1)S(1)} %get-tuple-element.175), channel_id=2, replica_groups=mesh['batch'=8,'head'=4] {'head'}, dimensions={0}, use_global_device_ids=true | all-gather | bytes 327680 | tf_op jit(solution)/shard_map/while/body/eval_jaxpr/all_gather | solution.py:93
  218.8 1.9 fusion.56
  221.5 5.8 %all-gather.3 = bf16[512,256]{1,0:T(8,128)(2,1)S(1)} all-gather(bf16[128,256]{1,0:T(8,128)(2,1)S(1)} %get-tuple-element.175), channel_id=2, replica_groups=mesh['batch'=8,'head'=4] {'head'}, dimensions={0}, use_global_device_ids=true | all-gather | bytes 327680 | tf_op jit(solution)/shard_map/while/body/eval_jaxpr/all_gather | solution.py:93
  227.8 1.9 fusion.56
  230.5 5.8 %all-gather.3 = bf16[512,256]{1,0:T(8,128)(2,1)S(1)} all-gather(bf16[128,256]{1,0:T(8,128)(2,1)S(1)} %get-tuple-element.175), channel_id=2, replica_groups=mesh['batch'=8,'head'=4] {'head'}, dimensions={0}, use_global_device_ids=true | all-gather | bytes 327680 | tf_op jit(solution)/shard_map/while/body/eval_jaxpr/all_gather | solution.py:93
  236.8 1.9 fusion.56
  239.5 5.8 %all-gather.3 = bf16[512,256]{1,0:T(8,128)(2,1)S(1)} all-gather(bf16[128,256]{1,0:T(8,128)(2,1)S(1)} %get-tuple-element.175), channel_id=2, replica_groups=mesh['batch'=8,'head'=4] {'head'}, dimensions={0}, use_global_device_ids=true | all-gather | bytes 327680 | tf_op jit(solution)/shard_map/while/body/eval_jaxpr/all_gather | solution.py:93
  248.5 5.8 %all-gather.3 = bf16[512,256]{1,0:T(8,128)(2,1)S(1)} all-gather(bf16[128,256]{1,0:T(8,128)(2,1)S(1)} %get-tuple-element.175), channel_id=2, replica_groups=mesh['batch'=8,'head'=4] {'head'}, dimensions={0}, use_global_device_ids=true | all-gather | bytes 327680 | tf_op jit(solution)/shard_map/while/body/eval_jaxpr/all_gather | solution.py:93
  254.8 1.9 fusion.56
  257.5 5.8 %all-gather.3 = bf16[512,256]{1,0:T(8,128)(2,1)S(1)} all-gather(bf16[128,256]{1,0:T(8,128)(2,1)S(1)} %get-tuple-element.175), channel_id=2, replica_groups=mesh['batch'=8,'head'=4] {'head'}, dimensions={0}, use_global_device_ids=true | all-gather | bytes 327680 | tf_op jit(solution)/shard_map/while/body/eval_jaxpr/all_gather | solution.py:93
  263.9 1.9 fusion.56
  266.6 5.8 %all-gather.3 = bf16[512,256]{1,0:T(8,128)(2,1)S(1)} all-gather(bf16[128,256]{1,0:T(8,128)(2,1)S(1)} %get-tuple-element.175), channel_id=2, replica_groups=mesh['batch'=8,'head'=4] {'head'}, dimensions={0}, use_global_device_ids=true | all-gather | bytes 327680 | tf_op jit(solution)/shard_map/while/body/eval_jaxpr/all_gather | solution.py:93
  275.6 5.8 %all-gather.3 = bf16[512,256]{1,0:T(8,128)(2,1)S(1)} all-gather(bf16[128,256]{1,0:T(8,128)(2,1)S(1)} %get-tuple-element.175), channel_id=2, replica_groups=mesh['batch'=8,'head'=4] {'head'}, dimensions={0}, use_global_device_ids=true | all-gather | bytes 327680 | tf_op jit(solution)/shard_map/while/body/eval_jaxpr/all_gather | solution.py:93
  281.9 1.9 fusion.56
  284.6 5.8 %all-gather.3 = bf16[512,256]{1,0:T(8,128)(2,1)S(1)} all-gather(bf16[128,256]{1,0:T(8,128)(2,1)S(1)} %get-tuple-element.175), channel_id=2, replica_groups=mesh['batch'=8,'head'=4] {'head'}, dimensions={0}, use_global_device_ids=true | all-gather | bytes 327680 | tf_op jit(solution)/shard_map/while/body/eval_jaxpr/all_gather | solution.py:93
  290.9 1.9 fusion.56
  293.6 5.8 %all-gather.3 = bf16[512,256]{1,0:T(8,128)(2,1)S(1)} all-gather(bf16[128,256]{1,0:T(8,128)(2,1)S(1)} %get-tuple-element.175), channel_id=2, replica_groups=mesh['batch'=8,'head'=4] {'head'}, dimensions={0}, use_global_device_ids=true | all-gather | bytes 327680 | tf_op jit(solution)/shard_map/while/body/eval_jaxpr/all_gather | solution.py:93
  299.9 1.9 fusion.56
  302.6 5.8 %all-gather.3 = bf16[512,256]{1,0:T(8,128)(2,1)S(1)} all-gather(bf16[128,256]{1,0:T(8,128)(2,1)S(1)} %get-tuple-element.175), channel_id=2, replica_groups=mesh['batch'=8,'head'=4] {'head'}, dimensions={0}, use_global_device_ids=true | all-gather | bytes 327680 | tf_op jit(solution)/shard_map/while/body/eval_jaxpr/all_gather | solution.py:93
  308.9 1.9 fusion.56
  311.6 5.8 %all-gather.3 = bf16[512,256]{1,0:T(8,128)(2,1)S(1)} all-gather(bf16[128,256]{1,0:T(8,128)(2,1)S(1)} %get-tuple-element.175), channel_id=2, replica_groups=mesh['batch'=8,'head'=4] {'head'}, dimensions={0}, use_global_device_ids=true | all-gather | bytes 327680 | tf_op jit(solution)/shard_map/while/body/eval_jaxpr/all_gather | solution.py:93
  317.9 1.9 fusion.56
  320.6 5.8 %all-gather.3 = bf16[512,256]{1,0:T(8,128)(2,1)S(1)} all-gather(bf16[128,256]{1,0:T(8,128)(2,1)S(1)} %get-tuple-element.175), channel_id=2, replica_groups=mesh['batch'=8,'head'=4] {'head'}, dimensions={0}, use_global_device_ids=true | all-gather | bytes 327680 | tf_op jit(solution)/shard_map/while/body/eval_jaxpr/all_gather | solution.py:93
  326.9 1.9 fusion.56
  329.6 5.8 %all-gather.3 = bf16[512,256]{1,0:T(8,128)(2,1)S(1)} all-gather(bf16[128,256]{1,0:T(8,128)(2,1)S(1)} %get-tuple-element.175), channel_id=2, replica_groups=mesh['batch'=8,'head'=4] {'head'}, dimensions={0}, use_global_device_ids=true | all-gather | bytes 327680 | tf_op jit(solution)/shard_map/while/body/eval_jaxpr/all_gather | solution.py:93
  335.9 1.9 fusion.56
  338.6 5.8 %all-gather.3 = bf16[512,256]{1,0:T(8,128)(2,1)S(1)} all-gather(bf16[128,256]{1,0:T(8,128)(2,1)S(1)} %get-tuple-element.175), channel_id=2, replica_groups=mesh['batch'=8,'head'=4] {'head'}, dimensions={0}, use_global_device_ids=true | all-gather | bytes 327680 | tf_op jit(solution)/shard_map/while/body/eval_jaxpr/all_gather | solution.py:93
  344.9 1.9 fusion.56
  347.6 5.8 %all-gather.3 = bf16[512,256]{1,0:T(8,128)(2,1)S(1)} all-gather(bf16[128,256]{1,0:T(8,128)(2,1)S(1)} %get-tuple-element.175), channel_id=2, replica_groups=mesh['batch'=8,'head'=4] {'head'}, dimensions={0}, use_global_device_ids=true | all-gather | bytes 327680 | tf_op jit(solution)/shard_map/while/body/eval_jaxpr/all_gather | solution.py:93
  353.9 1.9 fusion.56
  356.6 1.9 convert_bitcast_fusion
  360.1 3.9 all-to-all-start
  364.3 25.3 %all-to-all-done = bf16[32,8,16,256]{3,1,2,0:T(8,128)(2,1)S(1)} async-done(((bf16[32,8,16,256]{3,1,2,0:T(8,128)(2,1)}), bf16[32,8,16,256]{3,1,2,0:T(8,128)(2,1)S(1)}, u32[]{:S(2)}, u32[]{:S(2)}) %all-to-all-start) | async-done | bytes 2097184 | tf_op jit(solution)/shard_map/all_to_all | solution.py:105
  389.5 3.0 copy.88
  392.5 3.2 reshape.161
  395.8 8.2 %maximum_convert_fusion = bf16[8,128,1024]{2,1,0:T(8,128)(2,1)S(1)} fusion(bf16[8,128,1024]{2,1,0:T(8,128)(2,1)S(1)} %reshape.161, bf16[8,1024,1024]{2,1,0:T(8,128)(2,1)} %param.25), kind=kOutput, calls=%fused_computation.27 | convolution fusion | flops 2149580800 | bytes 20971520 | tf_op jit(solution)/shard_map/prh,phk->prk/dot_general | solution.py:108
  406.6 3.3 all-to-all-start.1
  409.9 3.9 all-to-all-done.1
  (173 shorter events, 50.3 us)
Async XLA Ops:
  7.2 396.8 %copy-start = (bf16[8,512,18]{1,0,2:T(8,128)(2,1)S(1)}, bf16[8,512,18]{1,0,2:T(8,128)(2,1)}, u32[]{:S(2)}) copy-start(bf16[8,512,18]{1,0,2:T(8,128)(2,1)} %param.27) | copy-start | bytes 442372
  7.2 46.0 %all-gather.10.cloned.1.call-start = ((), (), s32[]{:S(2)}) async-start(), calls=%async_computation.3 | async-start | bytes 1179648 | tf_op jit(solution)/shard_map/all_gather | solution.py:68
  7.9 95.2 %all-gather.12.cloned.1.call-start = ((), (), s32[]{:S(2)}) async-start(), calls=%async_computation.4 | async-start | bytes 2359296 | tf_op jit(solution)/shard_map/all_gather | solution.py:69
  8.7 123.1 %all-gather.8.cloned.1.call-start = ((), (), s32[]{:S(2)}) async-start(), calls=%async_computation.2 | async-start | bytes 3932160 | tf_op jit(solution)/shard_map/all_gather | solution.py:72
  360.1 3.9 copy-start.2
  360.1 29.4 %all-to-all-start = ((bf16[32,8,16,256]{3,1,2,0:T(8,128)(2,1)}), bf16[32,8,16,256]{3,1,2,0:T(8,128)(2,1)S(1)}, u32[]{:S(2)}, u32[]{:S(2)}) async-start(bf16[32,8,16,256]{3,1,2,0:T(8,128)(2,1)} %copy.61), calls=%async_computation | async-start | bytes 4194304 | tf_op jit(solution)/shard_map/all_to_all | solution.py:105
  395.8 8.6 %copy-start.3 = (bf16[8,512]{1,0:T(8,128)(2,1)S(1)}, bf16[8,512]{1,0:T(8,128)(2,1)}, u32[]{:S(2)}) copy-start(bf16[8,512]{1,0:T(8,128)(2,1)} %param.26) | copy-start | bytes 24580
  404.4 10.4 %copy-start.1 = (s32[32,16]{0,1:T(8,128)S(1)}, s32[32,16]{0,1:T(8,128)}, u32[]{:S(2)}) copy-start(s32[32,16]{0,1:T(8,128)} %param.21) | copy-start | bytes 6148
  406.6 7.2 %all-to-all-start.1 = ((bf16[4,2,2304]{2,1,0:T(2,128)(2,1)}), bf16[4,2,2304]{2,1,0:T(2,128)(2,1)S(1)}, u32[]{:S(2)}, u32[]{:S(2)}) async-start(bf16[4,2,2304]{2,1,0:T(2,128)(2,1)} %reshape.187), calls=%async_computation.1 | async-start | bytes 73728 | tf_op jit(solution)/shard_map/all_to_all | solution.py:119
Sparse Core Ops, SparseCore 0:
  10.1 42.9 all-gather.9
  55.3 47.7 all-gather.11
  104.7 27.0 all-gather.7
